TPU v7x, 16 devices: a 4x2x1 block of a 4x4x8 slice. The times are simulated.
16 devices in a mesh: rep: 2 (over y, z), data: 8 (over x, core).
Axes of the slice: x: 4, y: 2, z: 1, core: 2. Of those that a mesh axis runs over, the one named last changes fastest.
The devices are a block of a 4x4x8 slice.
Arguments:
- x: bfloat16 [4096, 3072], P(('rep', 'data')), parts along dimension 0
- adapter_id: int32 [4096], P(('rep', 'data')), parts along dimension 0
- dout: bfloat16 [4096, 3072], P(('rep', 'data')), parts along dimension 0
- w_gate: bfloat16 [3072, 8192], replicated
- w_up: bfloat16 [3072, 8192], replicated
- w_down: bfloat16 [8192, 3072], replicated
- a_gate: bfloat16 [128, 3072, 16], P('data')
- b_gate: bfloat16 [128, 16, 8192], P('data')
- a_up: bfloat16 [128, 3072, 16], P('data')
- b_up: bfloat16 [128, 16, 8192], P('data')
- a_down: bfloat16 [128, 8192, 16], P('data')
- b_down: bfloat16 [128, 16, 3072], P('data')
Outputs:
- output 1: bfloat16 [4096, 3072], P(('rep', 'data')), parts along dimension 0
- output 2: bfloat16 [4096, 3072], P(('rep', 'data')), parts along dimension 0
- output 3: float32 [256, 3072, 16], P(('rep', 'data')), parts along dimension 0
- output 4: float32 [256, 16, 8192], P(('rep', 'data')), parts along dimension 0
- output 5: float32 [256, 3072, 16], P(('rep', 'data')), parts along dimension 0
- output 6: float32 [256, 16, 8192], P(('rep', 'data')), parts along dimension 0
- output 7: float32 [256, 8192, 16], P(('rep', 'data')), parts along dimension 0
- output 8: float32 [256, 16, 3072], P(('rep', 'data')), parts along dimension 0
There are 2 independent parts. A program takes and returns all parts, laid end to end along the dimension named above; an argument that names none is the same for every part.
All inputs are finite; a program needn't handle non-finite values.
Results may differ from a plain program's by a relative error of at most 0.00139.
Values are sent between devices in bfloat16 or wider.
A program may use at most 768 MiB of HBM per device.

v0:
```python
import jax
import jax.numpy as jnp
from jax import lax
from jax.sharding import PartitionSpec as P

value_a10 = 32


def grouped_rows(in_rows, weight_set, group_sizes, contract_dim):
    dim_numbers = lax.RaggedDotDimensionNumbers(
        dot_dimension_numbers=(([1], [contract_dim]), ([], [])),
        lhs_ragged_dimensions=[0],
        rhs_group_dimensions=[0],
    )
    return lax.ragged_dot_general(in_rows, weight_set, group_sizes, dim_numbers, preferred_element_type=jnp.float32)


def grouped_outer(left_rows, right_rows, group_sizes):
    dim_numbers = lax.RaggedDotDimensionNumbers(
        dot_dimension_numbers=(([0], [0]), ([], [])),
        lhs_ragged_dimensions=[0],
        rhs_group_dimensions=[],
    )
    return lax.ragged_dot_general(left_rows, right_rows, group_sizes, dim_numbers, preferred_element_type=jnp.float32)


def contract_last(left_rows, weight):
    return lax.dot_general(left_rows, weight, (((1,), (1,)), ((), ())), preferred_element_type=jnp.float32)


def solution(mesh):
    group_size = mesh.shape['data']
    tok_spec = P(('rep', 'data'), None)
    id_spec = P(('rep', 'data'))
    full_spec = P(None, None)
    own_spec = P('data', None, None)
    grad_spec = P(('rep', 'data'), None, None)

    def device_fn(x_loc, ids_loc, dy_loc, w_gate, w_up, w_down, a_gate, b_gate, a_up, b_up, a_down, b_down):
        tokens = x_loc.shape[0]
        n_local = a_gate.shape[0]
        array_b10 = value_a10 / a_gate.shape[2]
        capacity = ((3 * tokens + 8 * group_size - 1) // (8 * group_size)) * 8
        owner_dev = ids_loc // n_local
        by_owner = jnp.argsort(owner_dev, stable=True)
        position = jnp.argsort(by_owner, stable=True)
        counts = jnp.bincount(owner_dev, length=group_size)
        starts = jnp.cumsum(counts) - counts
        dest_slot = owner_dev * capacity + position - starts[owner_dev]
        slot_token = jnp.full((group_size * capacity,), tokens, jnp.int32).at[dest_slot].set(jnp.arange(tokens, dtype=jnp.int32))

        def pack_rows(in_rows):
            return jnp.take(in_rows, slot_token, axis=0, mode='fill', fill_value=0)

        arrived_ids = lax.all_to_all(pack_rows(ids_loc % n_local), 'data', 0, 0, tiled=True)
        sort_order = jnp.argsort(arrived_ids, stable=True)
        restore = jnp.argsort(sort_order, stable=True)
        group_sizes = jnp.bincount(arrived_ids, length=n_local).astype(jnp.int32)

        def to_owner(in_rows):
            arrived = lax.all_to_all(pack_rows(in_rows), 'data', 0, 0, tiled=True)
            return jnp.take(arrived, sort_order, axis=0)

        def to_source(owner_rows):
            returned = lax.all_to_all(jnp.take(owner_rows, restore, axis=0), 'data', 0, 0, tiled=True)
            return jnp.take(returned, dest_slot, axis=0)

        x_own = to_owner(x_loc)
        p_gate = grouped_rows(x_own, a_gate, group_sizes, 1).astype(jnp.bfloat16)
        p_up = grouped_rows(x_own, a_up, group_sizes, 1).astype(jnp.bfloat16)
        e_gate = to_source((array_b10 * grouped_rows(p_gate, b_gate, group_sizes, 1)).astype(jnp.bfloat16))
        e_up = to_source((array_b10 * grouped_rows(p_up, b_up, group_sizes, 1)).astype(jnp.bfloat16))
        gate_pre = jnp.dot(x_loc, w_gate, preferred_element_type=jnp.float32) + e_gate.astype(jnp.float32)
        up_pre = jnp.dot(x_loc, w_up, preferred_element_type=jnp.float32) + e_up.astype(jnp.float32)
        gate_sig = jax.nn.sigmoid(gate_pre)
        gate_act = gate_pre * gate_sig
        hidden = (gate_act * up_pre).astype(jnp.bfloat16)
        h_own = to_owner(hidden)
        p_down = grouped_rows(h_own, a_down, group_sizes, 1).astype(jnp.bfloat16)
        e_down = to_source((array_b10 * grouped_rows(p_down, b_down, group_sizes, 1)).astype(jnp.bfloat16))
        out_loc = (x_loc.astype(jnp.float32) + jnp.dot(hidden, w_down, preferred_element_type=jnp.float32) + e_down.astype(jnp.float32)).astype(jnp.bfloat16)
        dy_own = to_owner(dy_loc)
        q_down = (array_b10 * grouped_rows(dy_own, b_down, group_sizes, 2)).astype(jnp.bfloat16)
        value_a7 = to_source(grouped_rows(q_down, a_down, group_sizes, 2).astype(jnp.bfloat16))
        grad_b_down = array_b10 * grouped_outer(p_down, dy_own, group_sizes)
        grad_a_down = grouped_outer(h_own, q_down, group_sizes)
        d_hidden = contract_last(dy_loc, w_down) + value_a7.astype(jnp.float32)
        d_gate = (d_hidden * up_pre * gate_sig * (1.0 + gate_pre * (1.0 - gate_sig))).astype(jnp.bfloat16)
        d_up = (d_hidden * gate_act).astype(jnp.bfloat16)
        dg_own = to_owner(d_gate)
        du_own = to_owner(d_up)
        q_gate = (array_b10 * grouped_rows(dg_own, b_gate, group_sizes, 2)).astype(jnp.bfloat16)
        q_up = (array_b10 * grouped_rows(du_own, b_up, group_sizes, 2)).astype(jnp.bfloat16)
        array_b7 = to_source((grouped_rows(q_gate, a_gate, group_sizes, 2) + grouped_rows(q_up, a_up, group_sizes, 2)).astype(jnp.bfloat16))
        grad_a_gate = grouped_outer(x_own, q_gate, group_sizes)
        grad_b_gate = array_b10 * grouped_outer(p_gate, dg_own, group_sizes)
        grad_a_up = grouped_outer(x_own, q_up, group_sizes)
        grad_b_up = array_b10 * grouped_outer(p_up, du_own, group_sizes)
        dx_loc = (dy_loc.astype(jnp.float32) + contract_last(d_gate, w_gate) + contract_last(d_up, w_up) + array_b7.astype(jnp.float32)).astype(jnp.bfloat16)
        return out_loc, dx_loc, grad_a_gate, grad_b_gate, grad_a_up, grad_b_up, grad_a_down, grad_b_down

    return jax.shard_map(
        device_fn,
        mesh=mesh,
        in_specs=(tok_spec, id_spec, tok_spec, full_spec, full_spec, full_spec, own_spec, own_spec, own_spec, own_spec, own_spec, own_spec),
        out_specs=(tok_spec, tok_spec, grad_spec, grad_spec, grad_spec, grad_spec, grad_spec, grad_spec),
        check_vma=False,
    )
```

profile of v0, /device:TPU:126, one launch (start us, length us, event | category | flops | bytes accessed | tf_op | source)
XLA Modules:
  0.0 2145.2 jit_solution(10623120908693226195)
XLA Ops:
  47.1 58.1 %all_to_all.129 = bf16[8,96,3072]{2,1,0:T(8,128)(2,1)} all-to-all(bf16[8,96,3072]{2,1,0:T(8,128)(2,1)} %bitcast.69), channel_id=1, replica_groups=mesh['rep'=2,'data'=8] {'data'}, dimensions={0} | all-to-all | bytes 9437184 | tf_op jit(solution)/shard_map/all_to_all | solution.py:61
  253.8 32.8 %ragged-dot-none.10 = f32[768,8192]{1,0:T(8,128)} custom-call(s32[1]{0:T(128)} %get-tuple-element.86, s32[17]{0:T(128)} %get-tuple-element.87, s32[18]{0:T(128)} %get-tuple-element.88, s32[18]{0:T(128)} %get-tuple-element.89, s32[1]{0:T(128)} %get-tuple-element.86, bf16[768,16]{1,0:T(8,128)(2,1)} %multiply_convert_fusion.8, bf16[16,16,8192]{2,1,0:T(8,128)(2,1)} %bitcast.70), custom_call_target="tpu_custom_call" | custom-call | flops 201326592 | bytes 29384768 | tf_op ragged-dot-none
  299.8 32.6 %ragged-dot-none.14 = f32[768,8192]{1,0:T(8,128)} custom-call(s32[1]{0:T(128)} %get-tuple-element.86, s32[17]{0:T(128)} %get-tuple-element.87, s32[18]{0:T(128)} %get-tuple-element.88, s32[18]{0:T(128)} %get-tuple-element.89, s32[1]{0:T(128)} %get-tuple-element.86, bf16[768,16]{1,0:T(8,128)(2,1)} %convert_element_type.73, bf16[16,16,8192]{2,1,0:T(8,128)(2,1)} %param.33), custom_call_target="tpu_custom_call" | custom-call | flops 201326592 | bytes 29384768 | tf_op jit(solution)/shard_map/ragged_dot_general/ragged-dot-none
  345.6 28.2 %gather_fusion.13 = bf16[768,8192]{1,0:T(8,128)(2,1)} fusion(bf16[768,8192]{1,0:T(8,128)(2,1)} %convert_element_type.83, s32[1024]{0:T(1024)S(1)} %pad_clamp_fusion.1), kind=kCustom, calls=%fused_computation.12.clone | custom fusion | bytes 25168896 | tf_op jit(solution)/shard_map/jit(_take)/gather | solution.py:65
  373.8 28.5 %gather_fusion.5 = bf16[768,8192]{1,0:T(8,128)(2,1)} fusion(bf16[768,8192]{1,0:T(8,128)(2,1)} %multiply_convert_fusion, s32[1024]{0:T(1024)S(1)} %pad_clamp_fusion.1), kind=kCustom, calls=%fused_computation.10.clone | custom fusion | bytes 25168896 | tf_op jit(solution)/shard_map/jit(_take)/gather | solution.py:65
  402.3 32.6 %ragged-dot-none.16 = f32[768,8192]{1,0:T(8,128)} custom-call(s32[1]{0:T(128)} %get-tuple-element.86, s32[17]{0:T(128)} %get-tuple-element.87, s32[18]{0:T(128)} %get-tuple-element.88, s32[18]{0:T(128)} %get-tuple-element.89, s32[1]{0:T(128)} %get-tuple-element.86, bf16[768,16]{1,0:T(8,128)(2,1)} %convert_element_type.70, bf16[16,16,8192]{2,1,0:T(8,128)(2,1)} %param.31), custom_call_target="tpu_custom_call" | custom-call | flops 201326592 | bytes 29384768 | tf_op jit(solution)/shard_map/ragged_dot_general/ragged-dot-none
  448.3 28.2 %gather_fusion.3 = bf16[768,8192]{1,0:T(8,128)(2,1)} fusion(bf16[768,8192]{1,0:T(8,128)(2,1)} %multiply_convert_fusion.1, s32[1024]{0:T(1024)S(1)} %pad_clamp_fusion.1), kind=kCustom, calls=%fused_computation.2.clone | custom fusion | bytes 25168896 | tf_op jit(solution)/shard_map/jit(_take)/gather | solution.py:65
  493.5 141.9 %all_to_all.130 = bf16[8,96,8192]{2,1,0:T(8,128)(2,1)} all-to-all(bf16[8,96,8192]{2,1,0:T(8,128)(2,1)S(1)} %bitcast.64), channel_id=1, replica_groups=mesh['rep'=2,'data'=8] {'data'}, dimensions={0} | all-to-all | bytes 25165824 | tf_op jit(solution)/shard_map/all_to_all | solution.py:65
  635.4 143.2 %all_to_all.131 = bf16[8,96,8192]{2,1,0:T(8,128)(2,1)} all-to-all(bf16[8,96,8192]{2,1,0:T(8,128)(2,1)S(1)} %bitcast.62), channel_id=1, replica_groups=mesh['rep'=2,'data'=8] {'data'}, dimensions={0} | all-to-all | bytes 25165824 | tf_op jit(solution)/shard_map/all_to_all | solution.py:65
  817.1 106.5 %all-to-all-done.2 = bf16[8,96,8192]{2,1,0:T(8,128)(2,1)} async-done(((bf16[8,96,8192]{2,1,0:T(8,128)(2,1)}), bf16[8,96,8192]{2,1,0:T(8,128)(2,1)}, u32[]{:S(2)}, u32[]{:S(2)}) %all-to-all-start.2) | async-done | bytes 12582944 | tf_op jit(solution)/shard_map/all_to_all | solution.py:65
  939.1 26.4 %convolution_add_fusion.2 = f32[256,8192]{1,0:T(8,128)} fusion(bf16[256,3072]{1,0:T(8,128)(2,1)S(1)} %copy-done.4, bf16[3072,8192]{1,0:T(8,128)(2,1)} %param.27, bf16[256,8192]{1,0:T(8,128)(2,1)} %gather_fusion.4, pred[256]{0:T(512)(128)(4,1)S(1)} %copy-done.25), kind=kOutput, calls=%fused_computation.37 | convolution fusion | flops 12891193344 | bytes 64487680 | tf_op jit(solution)/shard_map/dot_general | solution.py:73
  965.5 26.5 %convolution_add_fusion.1 = f32[256,8192]{1,0:T(8,128)} fusion(bf16[256,3072]{1,0:T(8,128)(2,1)S(1)} %copy-done.4, bf16[3072,8192]{1,0:T(8,128)(2,1)} %param.28, bf16[256,8192]{1,0:T(8,128)(2,1)} %gather_fusion.6, pred[256]{0:T(512)(128)(4,1)S(1)} %copy-done.25), kind=kOutput, calls=%fused_computation.36 | convolution fusion | flops 12891193344 | bytes 64487680 | tf_op jit(solution)/shard_map/dot_general | solution.py:74
  992.1 31.5 %multiply_convert_fusion.3 = (bf16[256,8192]{1,0:T(8,128)(2,1)}, bf16[256,8192]{1,0:T(8,128)(2,1)}, bf16[256,8192]{1,0:T(8,128)(2,1)}) fusion(f32[256,8192]{1,0:T(8,128)} %convolution_add_fusion.2, f32[256,8192]{1,0:T(8,128)} %convolution_add_fusion.1, bf16[256,8192]{1,0:T(8,128)(2,1)} %gather_fusion.14, pred[256]{0:T(512)(128)(4,1)S(1)} %copy-done.25, ...), kind=kOutput, calls=%fused_computation.40 | convolution fusion | flops 12922650624 | bytes 85459200 | tf_op jit(solution)/shard_map/dot_general | solution.py:28
  1115.4 143.3 %all_to_all.132 = bf16[8,96,8192]{2,1,0:T(8,128)(2,1)} all-to-all(bf16[8,96,8192]{2,1,0:T(8,128)(2,1)S(1)} %bitcast.63), channel_id=1, replica_groups=mesh['rep'=2,'data'=8] {'data'}, dimensions={0} | all-to-all | bytes 25165824 | tf_op jit(solution)/shard_map/all_to_all | solution.py:61
  1258.6 143.3 %all_to_all.133 = bf16[8,96,8192]{2,1,0:T(8,128)(2,1)} all-to-all(bf16[8,96,8192]{2,1,0:T(8,128)(2,1)S(1)} %bitcast.61), channel_id=1, replica_groups=mesh['rep'=2,'data'=8] {'data'}, dimensions={0} | all-to-all | bytes 25165824 | tf_op jit(solution)/shard_map/all_to_all | solution.py:61
  1479.6 28.2 %gather_fusion.16 = bf16[768,8192]{1,0:T(8,128)(2,1)} fusion(bf16[768,8192]{1,0:T(8,128)(2,1)} %bitcast.52, s32[1024]{0:T(1024)S(1)} %copy-done.14), kind=kCustom, calls=%fused_computation.13.clone | custom fusion | bytes 25168896 | tf_op jit(solution)/shard_map/jit(_take)/gather | solution.py:62
  1507.9 28.5 %gather_fusion.18 = bf16[768,8192]{1,0:T(8,128)(2,1)} fusion(bf16[768,8192]{1,0:T(8,128)(2,1)} %bitcast.53, s32[1024]{0:T(1024)S(1)} %copy-done.14), kind=kCustom, calls=%fused_computation.14.clone | custom fusion | bytes 25168896 | tf_op jit(solution)/shard_map/jit(_take)/gather | solution.py:62
  1547.0 28.3 %gather_fusion.8 = bf16[768,8192]{1,0:T(8,128)(2,1)} fusion(bf16[768,8192]{1,0:T(8,128)(2,1)} %bitcast.18, s32[1024]{0:T(1024)S(1)} %copy-done.14), kind=kCustom, calls=%fused_computation.11.clone | custom fusion | bytes 25168896 | tf_op jit(solution)/shard_map/jit(_take)/gather | solution.py:62
  1599.9 32.4 %ragged-dot-none.9 = f32[768,16]{1,0:T(8,128)} custom-call(s32[1]{0:T(128)} %get-tuple-element.86, s32[17]{0:T(128)} %get-tuple-element.87, s32[18]{0:T(128)} %get-tuple-element.88, s32[18]{0:T(128)} %get-tuple-element.89, s32[1]{0:T(128)} %get-tuple-element.86, bf16[768,8192]{1,0:T(8,128)(2,1)} %get-tuple-element.132, bf16[16,8192,16]{2,1,0:T(8,128)(2,1)} %bitcast.58), custom_call_target="tpu_custom_call" | custom-call | flops 201326592 | bytes 16826432 | tf_op ragged-dot-none
  1634.0 32.4 %ragged-dot-none.7 = f32[768,16]{1,0:T(8,128)} custom-call(s32[1]{0:T(128)} %get-tuple-element.86, s32[17]{0:T(128)} %get-tuple-element.87, s32[18]{0:T(128)} %get-tuple-element.88, s32[18]{0:T(128)} %get-tuple-element.89, s32[1]{0:T(128)} %get-tuple-element.86, bf16[768,8192]{1,0:T(8,128)(2,1)} %get-tuple-element.131, bf16[16,8192,16]{2,1,0:T(8,128)(2,1)} %bitcast.57), custom_call_target="tpu_custom_call" | custom-call | flops 201326592 | bytes 16826432 | tf_op ragged-dot-none
  1728.7 32.4 %ragged-dot-none.13 = f32[768,16]{1,0:T(8,128)} custom-call(s32[1]{0:T(128)} %get-tuple-element.86, s32[17]{0:T(128)} %get-tuple-element.87, s32[18]{0:T(128)} %get-tuple-element.88, s32[18]{0:T(128)} %get-tuple-element.89, s32[1]{0:T(128)} %get-tuple-element.86, bf16[768,8192]{1,0:T(8,128)(2,1)} %get-tuple-element.133, bf16[16,8192,16]{2,1,0:T(8,128)(2,1)} %copy.41), custom_call_target="tpu_custom_call" | custom-call | flops 201326592 | bytes 16826432 | tf_op jit(solution)/shard_map/ragged_dot_general/ragged-dot-none
  1900.0 25.2 %ragged-dot-none.5 = f32[16,3072,16]{2,1,0:T(8,128)} custom-call(s32[1]{0:T(128)} %get-tuple-element.42, s32[17]{0:T(128)} %get-tuple-element.43, s32[18]{0:T(128)} %get-tuple-element.44, s32[18]{0:T(128)} %get-tuple-element.45, s32[1]{0:T(128)} %get-tuple-element.42, bf16[768,3072]{1,0:T(8,128)(2,1)} %get-tuple-element.141, ...), custom_call_target="tpu_custom_call" | custom-call | flops 75497472 | bytes 7888960 | tf_op jit(solution)/shard_map/ragged_dot_general/ragged-dot-none
  1980.0 51.3 %ragged-dot-none.1 = f32[16,8192,16]{2,1,0:T(8,128)} custom-call(s32[1]{0:T(128)} %get-tuple-element.42, s32[17]{0:T(128)} %get-tuple-element.43, s32[18]{0:T(128)} %get-tuple-element.44, s32[18]{0:T(128)} %get-tuple-element.45, s32[1]{0:T(128)} %get-tuple-element.42, bf16[768,8192]{1,0:T(8,128)(2,1)} %get-tuple-element.133, ...), custom_call_target="tpu_custom_call" | custom-call | flops 201326592 | bytes 20996160 | tf_op jit(solution)/shard_map/ragged_dot_general/ragged-dot-none
  2031.2 36.7 %copy.47 = f32[16,8192,16]{1,2,0:T(8,128)} copy(f32[16,8192,16]{2,1,0:T(8,128)} %ragged-dot-none.1) | data formatting | bytes 16777216
  (156 shorter events, 845.0 us)
Async XLA Ops:
  0.6 28.3 %copy-start = (bf16[256,3072]{1,0:T(8,128)(2,1)S(1)}, bf16[256,3072]{1,0:T(8,128)(2,1)}, u32[]{:S(2)}) copy-start(bf16[256,3072]{1,0:T(8,128)(2,1)} %param.26) | copy-start | bytes 4718596
  18.6 15.3 copy-start.9
  23.6 15.2 copy-start.21
  24.3 22.8 %all-to-all-start.1 = ((s32[8,96,1]{1,2,0:T(1,128)}), s32[8,96,1]{1,2,0:T(1,128)S(1)}, u32[]{:S(2)}, u32[]{:S(2)}) async-start(s32[8,96,1]{1,2,0:T(1,128)} %bitcast.10), calls=%async_computation.1 | async-start | bytes 8192 | tf_op jit(solution)/shard_map/all_to_all | solution.py:55
  47.1 64.7 %copy-start.6 = (bf16[16,3072,16]{1,2,0:T(8,128)(2,1)S(1)}, bf16[16,3072,16]{1,2,0:T(8,128)(2,1)}, u32[]{:S(2)}) copy-start(bf16[16,3072,16]{1,2,0:T(8,128)(2,1)} %param.30) | copy-start | bytes 4718596
  105.2 62.7 %all-to-all-start.6 = ((bf16[8,96,3072]{2,1,0:T(8,128)(2,1)}), bf16[8,96,3072]{2,1,0:T(8,128)(2,1)}, u32[]{:S(2)}, u32[]{:S(2)}) async-start(bf16[8,96,3072]{2,1,0:T(8,128)(2,1)} %bitcast.66), calls=%async_computation.6 | async-start | bytes 9437184 | tf_op jit(solution)/shard_map/all_to_all | solution.py:61
  154.6 13.3 copy-start.13
  154.6 293.7 %copy-start.11 = (s32[1024]{0:T(1024)}, s32[1024]{0:T(1024)S(1)}, u32[]{:S(2)}) copy-start(s32[1024]{0:T(1024)S(1)} %pad_clamp_fusion.1) | copy-start | bytes 12292
  154.6 25.9 %copy-start.19 = (pred[768]{0:T(1024)(128)(4,1)}, pred[768]{0:T(1024)(128)(4,1)S(1)}, u32[]{:S(2)}) copy-start(pred[768]{0:T(1024)(128)(4,1)S(1)} %compare_and_fusion.1) | copy-start | bytes 2308
  448.3 28.2 %copy-start.17 = (pred[768]{0:T(1024)(128)(4,1)S(1)}, pred[768]{0:T(1024)(128)(4,1)}, u32[]{:S(2)}) copy-start(pred[768]{0:T(1024)(128)(4,1)} %compare_and_fusion) | copy-start | bytes 2308
  778.6 145.0 %all-to-all-start.2 = ((bf16[8,96,8192]{2,1,0:T(8,128)(2,1)}), bf16[8,96,8192]{2,1,0:T(8,128)(2,1)}, u32[]{:S(2)}, u32[]{:S(2)}) async-start(bf16[8,96,8192]{2,1,0:T(8,128)(2,1)} %bitcast.60), calls=%async_computation.2 | async-start | bytes 25165824 | tf_op jit(solution)/shard_map/all_to_all | solution.py:65
  786.4 137.2 %copy-start.15 = (s32[1024]{0:T(1024)}, s32[1024]{0:T(1024)S(1)}, u32[]{:S(2)}) copy-start(s32[1024]{0:T(1024)S(1)} %pad_clamp_fusion) | copy-start | bytes 12292
  923.6 15.5 copy-start.4
  923.6 15.5 copy-start.25
  965.5 26.5 %copy-start.1 = (bf16[256,3072]{1,0:T(8,128)(2,1)S(1)}, bf16[256,3072]{1,0:T(8,128)(2,1)}, u32[]{:S(2)}) copy-start(bf16[256,3072]{1,0:T(8,128)(2,1)} %param.26) | copy-start | bytes 4718596
  992.1 31.5 %copy-start.10 = (s32[1024]{0:T(1024)S(1)}, s32[1024]{0:T(1024)}, u32[]{:S(2)}) copy-start(s32[1024]{0:T(1024)} %copy-done.9) | copy-start | bytes 12292
  1073.3 24.9 %copy-start.22 = (pred[768]{0:T(1024)(128)(4,1)S(1)}, pred[768]{0:T(1024)(128)(4,1)}, u32[]{:S(2)}) copy-start(pred[768]{0:T(1024)(128)(4,1)} %copy-done.21) | copy-start | bytes 2308
  1401.9 145.1 %all-to-all-start.4 = ((bf16[8,96,8192]{2,1,0:T(8,128)(2,1)}), bf16[8,96,8192]{2,1,0:T(8,128)(2,1)}, u32[]{:S(2)}, u32[]{:S(2)}) async-start(bf16[8,96,8192]{2,1,0:T(8,128)(2,1)} %bitcast.59), calls=%async_computation.4 | async-start | bytes 25165824 | tf_op jit(solution)/shard_map/all_to_all | solution.py:61
  1456.3 23.3 %copy-start.14 = (s32[1024]{0:T(1024)S(1)}, s32[1024]{0:T(1024)}, u32[]{:S(2)}) copy-start(s32[1024]{0:T(1024)} %copy-done.13) | copy-start | bytes 12292
  1547.0 28.3 %copy-start.20 = (pred[768]{0:T(1024)(128)(4,1)S(1)}, pred[768]{0:T(1024)(128)(4,1)}, u32[]{:S(2)}) copy-start(pred[768]{0:T(1024)(128)(4,1)} %copy-done.19) | copy-start | bytes 2308
  1789.2 12.7 copy-start.18
  1810.3 73.8 %all-to-all-start.5 = ((bf16[8,96,3072]{2,1,0:T(8,128)(2,1)}), bf16[8,96,3072]{2,1,0:T(8,128)(2,1)}, u32[]{:S(2)}, u32[]{:S(2)}) async-start(bf16[8,96,3072]{2,1,0:T(8,128)(2,1)} %bitcast.68), calls=%async_computation.5 | async-start | bytes 9437184 | tf_op jit(solution)/shard_map/all_to_all | solution.py:65
  1884.1 232.1 %all-to-all-start.10 = ((bf16[8,96,3072]{2,1,0:T(8,128)(2,1)}), bf16[8,96,3072]{2,1,0:T(8,128)(2,1)}, u32[]{:S(2)}, u32[]{:S(2)}) async-start(bf16[8,96,3072]{2,1,0:T(8,128)(2,1)} %bitcast.67), calls=%async_computation.10 | async-start | bytes 9437184 | tf_op jit(solution)/shard_map/all_to_all | solution.py:65
  2068.0 18.7 copy-start.16
  (9 other events, 58.8 us)
where the time goes:
time: 2160 us; the launch traced here: 2150 us
  blocking collectives  630 us (29%)
  local copies, waits for them, and re-layouts  533 us (25%)
  Pallas kernels  477 us (22%)
  other arithmetic  198 us (9%)
  matrix products  153 us (7%)
  waiting for transfers between devices  117 us (5%)
  starting transfers between devices  36.4 us (2%)
    all_to_all x3, blocking collectives, to_owner(): arrived = lax.all_to_all(pack_rows(in_rows), 'data', 0, 0, tiled=True)  345 us
    another operation x12, Pallas kernels  318 us
    all_to_all x2, blocking collectives, to_source(): lax.all_to_all(jnp.take(owner_rows, restore, axis=0), 'data', 0, 0, tiled...  285 us
    unnamed x63, local copies, waits for them, and re-layouts  161 us
    unnamed x8, Pallas kernels  159 us
    gather x5, local copies, waits for them, and re-layouts, to_owner(): return jnp.take(arrived, sort_order, axis=0)  110 us
    gather x5, local copies, waits for them, and re-layouts, to_source(): jnp.take(owner_rows, restore, axis=0)  110 us
    all_to_all x3, waiting for transfers between devices, to_source(): lax.all_to_all(jnp.take(owner_rows, restore, axis=0), 'data', 0, 0, tiled...  106 us
  transfers between devices with their start and end apart: 6, of which 2 were waited for; matrix products, arithmetic and copies ran while one was open for 17% of the time, Pallas kernels for 8%

commit v1 on v0

v1 whole, which is shorter than its diff:
```python
import functools

import jax
import jax.numpy as jnp
from jax import lax
from jax.experimental import pallas as pl
from jax.experimental.pallas import tpu as pltpu
from jax.sharding import PartitionSpec as P

ALPHA = 32
LANES = 128
VMEM_LIMIT = 60 * 1024 * 1024


def mm(a, b):
    return lax.dot_general(a, b, (((1,), (0,)), ((), ())), preferred_element_type=jnp.float32)


def mmt(a, b):
    return lax.dot_general(a, b, (((1,), (1,)), ((), ())), preferred_element_type=jnp.float32)


def tmm(a, b):
    return lax.dot_general(a, b, (((0,), (0,)), ((), ())), preferred_element_type=jnp.float32)


def bf(v):
    return v.astype(jnp.bfloat16)


def pack_kernel(cap, slot_ref, x_ref, d_ref, id_ref, *outs):
    dim = x_ref.shape[1]
    tokens = x_ref.shape[0]
    row = lax.broadcasted_iota(jnp.int32, (cap, tokens), 0)
    slot = slot_ref[...]
    for q, out in enumerate(outs):
        pick = jnp.where(slot == row + q * cap, 1.0, 0.0).astype(jnp.bfloat16)
        out[:, :dim] = bf(mm(pick, x_ref[...]))
        out[:, dim:2 * dim] = bf(mm(pick, d_ref[...]))
        out[:, 2 * dim:] = bf(mm(pick, id_ref[...]))


def pack_rows(slot_row, x, d, ids, n, cap):
    tokens, dim = x.shape
    return pl.pallas_call(
        functools.partial(pack_kernel, cap),
        out_shape=[jax.ShapeDtypeStruct((cap, 2 * dim + LANES), jnp.bfloat16)] * n,
        in_specs=[pl.BlockSpec(memory_space=pltpu.VMEM)] * 4,
        out_specs=[pl.BlockSpec(memory_space=pltpu.VMEM)] * n,
        compiler_params=pltpu.CompilerParams(vmem_limit_bytes=VMEM_LIMIT),
        cost_estimate=pl.CostEstimate(flops=2 * n * cap * tokens * 2 * dim, bytes_accessed=4 * dim * (tokens + n * cap), transcendentals=0),
        name="pack",
    )(slot_row, x, d, ids)


def unpack_kernel(n, cap, slot_ref, *refs):
    outs = refs[2 * n:]
    tokens = slot_ref.shape[0]
    col = lax.broadcasted_iota(jnp.int32, (tokens, n * cap), 1)
    pick = jnp.where(slot_ref[...] == col, 1.0, 0.0).astype(jnp.bfloat16)
    for k in range(2):
        rows = jnp.concatenate([r[...] for r in refs[k * n:(k + 1) * n]], axis=0)
        outs[k][...] = bf(mm(pick, rows))


def unpack_rows(slot_col, parts, cap):
    n = len(parts)
    tokens = slot_col.shape[0]
    dim = parts[0].shape[1] // 2
    width = dim // 3
    steps = dim // width
    return pl.pallas_call(
        functools.partial(unpack_kernel, n, cap),
        grid=(steps,),
        out_shape=[jax.ShapeDtypeStruct((tokens, dim), jnp.bfloat16)] * 2,
        in_specs=[pl.BlockSpec((tokens, 1), lambda j: (0, 0))]
        + [pl.BlockSpec((cap, width), lambda j: (0, j))] * n
        + [pl.BlockSpec((cap, width), lambda j: (0, j + steps))] * n,
        out_specs=[pl.BlockSpec((tokens, width), lambda j: (0, j))] * 2,
        compiler_params=pltpu.CompilerParams(vmem_limit_bytes=VMEM_LIMIT),
        cost_estimate=pl.CostEstimate(flops=2 * n * cap * tokens * 2 * dim, bytes_accessed=4 * dim * (tokens + n * cap), transcendentals=0),
        name="unpack",
    )(slot_col, *parts, *parts)


def layer_kernel(nb, scale, rank, *refs):
    bufs = refs[:nb]
    ag, au, bd, wg, wu, wd, bg, bu, ad = refs[nb:nb + 9]
    res = refs[nb + 9:2 * nb + 9]
    h_out, dg_out, du_out, pq = refs[2 * nb + 9:2 * nb + 13]
    xs, ds, acc_o, acc_x, accp, mask = refs[2 * nb + 13:]
    step = pl.program_id(0)
    cap = bufs[0].shape[0]
    dim = xs.shape[1]
    cols = mask.shape[1]

    @pl.when(step == 0)
    def _():
        for i, b in enumerate(bufs):
            rows = pl.ds(i * cap, cap)
            xs[rows, :] = b[:, :dim]
            ds[rows, :] = b[:, dim:2 * dim]
            aid = b[:, 2 * dim:2 * dim + 1].astype(jnp.float32)
            col = (lax.broadcasted_iota(jnp.int32, (cap, cols), 1) // rank + 1).astype(jnp.float32)
            mask[rows, :] = jnp.where(aid == col, 1.0, 0.0)
        keep = mask[...] > 0.5
        pq[0] = bf(jnp.where(keep, mmt(xs[...], ag[...]), 0.0))
        pq[1] = bf(jnp.where(keep, mmt(xs[...], au[...]), 0.0))
        pq[2] = bf(jnp.where(keep, scale * mmt(ds[...], bd[...]), 0.0))
        acc_o[...] = jnp.zeros_like(acc_o)
        acc_x[...] = jnp.zeros_like(acc_x)
        accp[...] = jnp.zeros_like(accp)

    eg = bf(scale * mm(pq[0], bg[...])).astype(jnp.float32)
    eu = bf(scale * mm(pq[1], bu[...])).astype(jnp.float32)
    el = bf(mm(pq[2], ad[...])).astype(jnp.float32)
    g = mm(xs[...], wg[...]) + eg
    u = mm(xs[...], wu[...]) + eu
    dh = mmt(ds[...], wd[...]) + el
    sig = jax.nn.sigmoid(g)
    act = g * sig
    h = bf(act * u)
    dg = bf(dh * u * sig * (1.0 + g * (1.0 - sig)))
    du = bf(dh * act)
    h_out[...] = h
    dg_out[...] = dg
    du_out[...] = du
    acc_o[...] += mm(h, wd[...])
    acc_x[...] += mmt(dg, wg[...]) + mmt(du, wu[...])
    accp[0] += mmt(h, ad[...])
    accp[1] += mmt(dg, bg[...])
    accp[2] += mmt(du, bu[...])

    @pl.when(step == pl.num_programs(0) - 1)
    def _():
        keep = mask[...] > 0.5
        pd = bf(jnp.where(keep, accp[0], 0.0))
        qg = bf(jnp.where(keep, scale * accp[1], 0.0))
        qu = bf(jnp.where(keep, scale * accp[2], 0.0))
        pq[3] = pd
        pq[4] = qg
        pq[5] = qu
        ed = bf(scale * mm(pd, bd[...])).astype(jnp.float32)
        out = bf(xs[...].astype(jnp.float32) + acc_o[...] + ed)
        dl = bf(mm(qg, ag[...]) + mm(qu, au[...])).astype(jnp.float32)
        dx = bf(ds[...].astype(jnp.float32) + acc_x[...] + dl)
        for i, r in enumerate(res):
            r[:, :dim] = out[i * cap:(i + 1) * cap]
            r[:, dim:] = dx[i * cap:(i + 1) * cap]


def layer(bufs, ag, au, bd, wg, wu, wd, bg, bu, ad, rank, tile, name):
    nb = len(bufs)
    cap = bufs[0].shape[0]
    rows = nb * cap
    dim, hid = wg.shape
    cols = ag.shape[0]
    once = pl.Buffered(1)
    fixed = lambda shape: pl.BlockSpec(shape, lambda f: (0,) * len(shape), pipeline_mode=once)
    flops = 2 * rows * (6 * dim * hid + 6 * cols * (dim + hid))
    byts = 2 * (3 * dim * hid + 3 * cols * (dim + hid) + rows * (4 * dim + 3 * hid))
    out = pl.pallas_call(
        functools.partial(layer_kernel, nb, ALPHA / rank, rank),
        grid=(hid // tile,),
        out_shape=[jax.ShapeDtypeStruct((cap, 2 * dim), jnp.bfloat16)] * nb
        + [jax.ShapeDtypeStruct((rows, hid), jnp.bfloat16)] * 3
        + [jax.ShapeDtypeStruct((6, rows, cols), jnp.bfloat16)],
        in_specs=[fixed((cap, 2 * dim + LANES))] * nb
        + [fixed((cols, dim))] * 3
        + [pl.BlockSpec((dim, tile), lambda f: (0, f))] * 2
        + [pl.BlockSpec((tile, dim), lambda f: (f, 0))]
        + [pl.BlockSpec((cols, tile), lambda f: (0, f))] * 3,
        out_specs=[fixed((cap, 2 * dim))] * nb
        + [pl.BlockSpec((rows, tile), lambda f: (0, f))] * 3
        + [fixed((6, rows, cols))],
        scratch_shapes=[
            pltpu.VMEM((rows, dim), jnp.bfloat16),
            pltpu.VMEM((rows, dim), jnp.bfloat16),
            pltpu.VMEM((rows, dim), jnp.float32),
            pltpu.VMEM((rows, dim), jnp.float32),
            pltpu.VMEM((3, rows, cols), jnp.float32),
            pltpu.VMEM((rows, cols), jnp.float32),
        ],
        compiler_params=pltpu.CompilerParams(vmem_limit_bytes=VMEM_LIMIT),
        cost_estimate=pl.CostEstimate(flops=flops, bytes_accessed=byts, transcendentals=rows * hid),
        name=name,
    )(*bufs, ag, au, bd, wg, wu, wd, bg, bu, ad)
    return out[:nb], out[nb:nb + 3], out[nb + 3]


def grad_f_kernel(ns, scale, *refs):
    pqs = refs[:ns]
    hs, dgs, dus = refs[ns:2 * ns], refs[2 * ns:3 * ns], refs[3 * ns:4 * ns]
    gbg, gbu, gad = refs[4 * ns:]
    cat = lambda vs: jnp.concatenate(vs, axis=0)
    gbg[...] = scale * tmm(cat([p[0] for p in pqs]), cat([r[...] for r in dgs]))
    gbu[...] = scale * tmm(cat([p[1] for p in pqs]), cat([r[...] for r in dus]))
    gad[...] = tmm(cat([p[2] for p in pqs]), cat([r[...] for r in hs]))


def grad_f(pqs, hs, dgs, dus, scale, tile):
    ns = len(pqs)
    cols = pqs[0].shape[2]
    hid = hs[0].shape[1]
    rows = [p.shape[1] for p in pqs]
    return pl.pallas_call(
        functools.partial(grad_f_kernel, ns, scale),
        grid=(hid // tile,),
        out_shape=[jax.ShapeDtypeStruct((cols, hid), jnp.float32)] * 3,
        in_specs=[pl.BlockSpec((6, m, cols), lambda f: (0, 0, 0)) for m in rows]
        + [pl.BlockSpec((m, tile), lambda f: (0, f)) for m in rows] * 3,
        out_specs=[pl.BlockSpec((cols, tile), lambda f: (0, f))] * 3,
        compiler_params=pltpu.CompilerParams(vmem_limit_bytes=VMEM_LIMIT),
        cost_estimate=pl.CostEstimate(flops=6 * cols * sum(rows) * hid, bytes_accessed=6 * hid * (sum(rows) + 2 * cols), transcendentals=0),
        name="grad_hidden",
    )(*pqs, *hs, *dgs, *dus)


def grad_d_kernel(ns, nb, scale, *refs):
    pqs = refs[:ns]
    xs, ds = refs[ns:ns + nb], refs[ns + nb:ns + 2 * nb]
    gag, gau, gbd = refs[ns + 2 * nb:]
    cat = lambda vs: jnp.concatenate(vs, axis=0)
    x = cat([r[...] for r in xs])
    gag[...] = tmm(cat([p[4] for p in pqs]), x)
    gau[...] = tmm(cat([p[5] for p in pqs]), x)
    gbd[...] = scale * tmm(cat([p[3] for p in pqs]), cat([r[...] for r in ds]))


def grad_d(pqs, bufs, dim, scale, tile):
    ns, nb = len(pqs), len(bufs)
    cols = pqs[0].shape[2]
    cap = bufs[0].shape[0]
    steps = dim // tile
    rows = [p.shape[1] for p in pqs]
    return pl.pallas_call(
        functools.partial(grad_d_kernel, ns, nb, scale),
        grid=(steps,),
        out_shape=[jax.ShapeDtypeStruct((cols, dim), jnp.float32)] * 3,
        in_specs=[pl.BlockSpec((6, m, cols), lambda f: (0, 0, 0)) for m in rows]
        + [pl.BlockSpec((cap, tile), lambda f: (0, f))] * nb
        + [pl.BlockSpec((cap, tile), lambda f: (0, f + steps))] * nb,
        out_specs=[pl.BlockSpec((cols, tile), lambda f: (0, f))] * 3,
        compiler_params=pltpu.CompilerParams(vmem_limit_bytes=VMEM_LIMIT),
        cost_estimate=pl.CostEstimate(flops=6 * cols * sum(rows) * dim, bytes_accessed=4 * dim * (sum(rows) + 3 * cols), transcendentals=0),
        name="grad_model",
    )(*pqs, *bufs, *bufs)


def solution(mesh):
    n = mesh.shape['data']
    chips = n // 2
    tok_spec = P(('rep', 'data'), None)
    id_spec = P(('rep', 'data'))
    full_spec = P(None, None)
    own_spec = P('data', None, None)
    grad_spec = P(('rep', 'data'), None, None)
    hops = [0, 1, chips - 1] + list(range(2, chips - 1))
    place = [hops.index(r) for r in range(chips)]

    def there(r, b):
        return [(i, (i // 2 + r) % chips * 2 + (i % 2 ^ b)) for i in range(n)]

    def send(v, r, b):
        return v if r == 0 and b == 0 else lax.ppermute(v, 'data', there(r, b))

    def back(v, r, b):
        return v if r == 0 and b == 0 else lax.ppermute(v, 'data', [(d, s) for s, d in there(r, b)])

    def device_fn(x, ids, dy, w_gate, w_up, w_down, a_gate, b_gate, a_up, b_up, a_down, b_down):
        tokens, dim = x.shape
        hid = w_gate.shape[1]
        n_local, _, rank = a_gate.shape
        cols = n_local * rank
        scale = ALPHA / rank
        cap = ((3 * tokens + 8 * n - 1) // (8 * n)) * 8
        me = lax.axis_index('data')

        ag = a_gate.transpose(0, 2, 1).reshape(cols, dim)
        au = a_up.transpose(0, 2, 1).reshape(cols, dim)
        ad = a_down.transpose(0, 2, 1).reshape(cols, hid)
        bg = b_gate.reshape(cols, hid)
        bu = b_up.reshape(cols, hid)
        bd = b_down.reshape(cols, dim)

        owner = ids // n_local
        rel = (owner // 2 - me // 2) % chips
        pos = jnp.zeros_like(rel)
        for r in range(chips):
            pos = jnp.where(rel == r, place[r], pos)
        pos = 2 * pos + (owner % 2 + me % 2) % 2
        t = jnp.arange(tokens, dtype=jnp.int32)
        before = (owner[:, None] == owner[None, :]) & (t[None, :] < t[:, None])
        slot = pos * cap + jnp.sum(before.astype(jnp.int32), axis=1)
        idc = jnp.broadcast_to((ids % n_local + 1)[:, None], (tokens, LANES)).astype(jnp.bfloat16)

        packed = pack_rows(slot[None, :], x, dy, idc, n, cap)

        def stage(bufs, name):
            return layer(bufs, ag, au, bd, w_gate, w_up, w_down, bg, bu, ad, rank, 512, name)

        groups = [[0], [1, 2], list(range(3, chips))]
        got = [None] * n
        for p in range(6):
            got[p] = send(packed[p], hops[p // 2], p % 2)
        res0, hid0, pq0 = stage(got[0:2], "layer_own")
        late, _ = lax.optimization_barrier((tuple(packed[6:]), pq0))
        for p in range(6, n):
            got[p] = send(late[p - 6], hops[p // 2], p % 2)
        res1, hid1, pq1 = stage(got[2:6], "layer_near")
        res2, hid2, pq2 = stage(got[6:], "layer_far")
        res = list(res0) + list(res1) + list(res2)
        parts = [back(res[p], hops[p // 2], p % 2) for p in range(n)]

        pqs = [pq0, pq1, pq2]
        hids = [hid0, hid1, hid2]
        gbg, gbu, gad = grad_f(pqs, [v[0] for v in hids], [v[1] for v in hids], [v[2] for v in hids], scale, 512)
        gag, gau, gbd = grad_d(pqs, got, dim, scale, 512)
        out, dx = unpack_rows(slot[:, None], parts, cap)

        def as_a(v):
            return v.reshape(n_local, rank, v.shape[1]).transpose(0, 2, 1)

        def as_b(v):
            return v.reshape(n_local, rank, v.shape[1])

        return out, dx, as_a(gag), as_b(gbg), as_a(gau), as_b(gbu), as_a(gad), as_b(gbd)

    return jax.shard_map(
        device_fn,
        mesh=mesh,
        in_specs=(tok_spec, id_spec, tok_spec, full_spec, full_spec, full_spec, own_spec, own_spec, own_spec, own_spec, own_spec, own_spec),
        out_specs=(tok_spec, tok_spec, grad_spec, grad_spec, grad_spec, grad_spec, grad_spec, grad_spec),
        check_vma=False,
    )
```

time: 2160 us -> 442 us (0.20)
  blocking collectives: 630 us -> 0 us
  local copies, waits for them, and re-layouts: 533 us -> 2.57 us
  other arithmetic: 198 us -> 1.44 us
  matrix products: 153 us -> 0 us
  waiting for transfers between devices: 117 us -> 13.4 us
  Pallas kernels: 477 us -> 407 us
    all_to_all x5 -> x0, blocking collectives: 630 us -> none  [the longest x3 345 us: to_owner(): arrived = lax.all_to_all(pack_rows(in_rows), 'data', 0, 0, tiled=True)]
    pallas_call x0 -> x7, Pallas kernels: none -> 407 us  [the longest x3 354 us: layer(): pl.pallas_call(functools.partial(layer_kernel, nb, ALPHA / rank, rank), g...]
    gather x22 -> x0, local copies, waits for them, and re-layouts: 369 us -> none  [the longest x5 110 us: to_owner(): return jnp.take(arrived, sort_order, axis=0)]
    another operation x12 -> x0, Pallas kernels: 318 us -> none
    unnamed x63 -> x14, local copies, waits for them, and re-layouts: 161 us -> 1.04 us
    unnamed x8 -> x0, Pallas kernels: 159 us -> none
    dot_general x6 -> x0, matrix products: 153 us -> none  [the longest x3 76.8 us: contract_last(): lax.dot_general(left_rows, weight, (((1,), (1,)), ((), ())), preferred_el...]
    all_to_all x6 -> x0, waiting for transfers between devices: 117 us -> none  [the longest x3 106 us: to_source(): lax.all_to_all(jnp.take(owner_rows, restore, axis=0), 'data', 0, 0, tiled...]
  transfers between devices with their start and end apart: 6 -> 14, of which waited for: 2 -> 1; matrix products, arithmetic and copies ran while one was open for 17% -> 0% of each run, Pallas kernels for 8% -> 89%
where the time goes in v1:
time: 442 us; the launch traced here: 440 us
  Pallas kernels  407 us (92%)
  starting transfers between devices  15.4 us (3%)
  waiting for transfers between devices  13.4 us (3%)
    pallas_call x3, Pallas kernels, layer(): pl.pallas_call(functools.partial(layer_kernel, nb, ALPHA / rank, rank), g...  354 us
    pallas_call x1, Pallas kernels, grad_f(): pl.pallas_call(functools.partial(grad_f_kernel, ns, scale), grid=(hid //...  27.7 us
    ppermute x7, waiting for transfers between devices, back(): lax.ppermute(v, 'data', [(d, s) for s, d in there(r, b)])  13.4 us
    pallas_call x1, Pallas kernels, grad_d(): pl.pallas_call(functools.partial(grad_d_kernel, ns, nb, scale), grid=(ste...  10.7 us
    ppermute x7, starting transfers between devices, back(): lax.ppermute(v, 'data', [(d, s) for s, d in there(r, b)])  8.95 us
  transfers between devices with their start and end apart: 14, of which 1 were waited for; matrix products, arithmetic and copies ran while one was open for 0% of the time, Pallas kernels for 89%

profile of v1, /device:TPU:126, one launch (start us, length us, event | category | flops | bytes accessed | tf_op | source)
XLA Modules:
  0.0 440.4 jit_solution(5885781753993256008)
XLA Ops:
  0.6 0.7 fusion.7
  2.1 0.7 broadcast_in_dim.23.id_ref
  2.8 7.1 %pack.1 = (bf16[96,6272]{1,0:T(8,128)(2,1)}, bf16[96,6272]{1,0:T(8,128)(2,1)}, bf16[96,6272]{1,0:T(8,128)(2,1)}, bf16[96,6272]{1,0:T(8,128)(2,1)}, bf16[96,6272]...) custom-call(s32[1,256]{1,0:T(1,128)} %bitcast.26, ...), custom_call_target="tpu_custom_call" | custom-call | flops 2415919104 | bytes 12582912 | tf_op jit(solution)/shard_map/pack/pallas_call | solution.py:45
  10.0 1.5 collective-permute-start.3
  11.5 0.6 collective-permute-start.4
  12.1 1.4 collective-permute-start.5
  13.4 0.8 copy.21.slot_ref
  14.2 1.0 copy-done
  15.2 101.8 %layer_own.1 = (bf16[96,6144]{1,0:T(8,128)(2,1)}, bf16[96,6144]{1,0:T(8,128)(2,1)}, bf16[192,8192]{1,0:T(8,128)(2,1)}, bf16[192,8192]{1,0:T(8,128)(2,1)}, bf16[1...) custom-call(bf16[96,6272]{1,0:T(8,128)(2,1)} %get-tuple-element.46.refs_0_.refs_3_.refs_11_, bf16[96,6272]{1,0:T(8,128)(2,1)} %copy-done, ...), custom_call_target="tpu_custom_call" | custom-call | flops 64625836032 | bytes 182452224 | tf_op jit(solution)/shard_map/layer_own/pallas_call | solution.py:162
  117.0 0.6 collective-permute-start.1
  117.6 2.3 collective-permute-start.10
  119.9 0.6 collective-permute-start.11
  120.6 150.2 %layer_near.1 = (bf16[96,6144]{1,0:T(8,128)(2,1)}, bf16[96,6144]{1,0:T(8,128)(2,1)}, bf16[96,6144]{1,0:T(8,128)(2,1)}, bf16[96,6144]{1,0:T(8,128)(2,1)}, bf16[38...) custom-call(bf16[96,6272]{1,0:T(8,128)(2,1)} %copy-done.1, ...), custom_call_target="tpu_custom_call" | custom-call | flops 129251672064 | bytes 196608000 | tf_op jit(solution)/shard_map/layer_near/pallas_call | solution.py:162
  270.8 0.8 collective-permute-start.6
  271.5 1.6 collective-permute-start.7
  273.2 1.6 collective-permute-start.8
  274.8 0.8 collective-permute-start.9
  275.6 101.8 %layer_far.1 = (bf16[96,6144]{1,0:T(8,128)(2,1)}, bf16[96,6144]{1,0:T(8,128)(2,1)}, bf16[192,8192]{1,0:T(8,128)(2,1)}, bf16[192,8192]{1,0:T(8,128)(2,1)}, bf16[1...) custom-call(bf16[96,6272]{1,0:T(8,128)(2,1)} %copy-done.2, ...), custom_call_target="tpu_custom_call" | custom-call | flops 64625836032 | bytes 182452224 | tf_op jit(solution)/shard_map/layer_far/pallas_call | solution.py:162
  377.3 1.2 collective-permute-start.12
  378.5 2.4 collective-permute-start.13
  380.9 10.7 %grad_model.1 = (f32[256,3072]{1,0:T(8,128)}, f32[256,3072]{1,0:T(8,128)}, f32[256,3072]{1,0:T(8,128)}) custom-call(bf16[6,192,256]{2,1,0:T(8,128)(2,1)} %get-tuple-element.60.refs_0_, bf16[6,384,256]{2,1,0:T(8,128)(2,1)} %get-tuple-element.67.refs_1_, bf16[6,192,256]{2,1,0:T(8,128)(2,1)} %get-tuple-element.68.refs_2_, ...), custom_call_target="tpu_custom_call" | custom-call | flops 3623878656 | bytes 18874368 | tf_op jit(solution)/shard_map/grad_model/pallas_call | solution.py:236
  391.6 27.7 %grad_hidden.1 = (f32[256,8192]{1,0:T(8,128)}, f32[256,8192]{1,0:T(8,128)}, f32[256,8192]{1,0:T(8,128)}) custom-call(bf16[6,192,256]{2,1,0:T(8,128)(2,1)} %get-tuple-element.60.refs_0_, bf16[6,384,256]{2,1,0:T(8,128)(2,1)} %get-tuple-element.67.refs_1_, bf16[6,192,256]{2,1,0:T(8,128)(2,1)} %get-tuple-element.68.refs_2_, ...), custom_call_target="tpu_custom_call" | custom-call | flops 9663676416 | bytes 62914560 | tf_op jit(solution)/shard_map/grad_hidden/pallas_call | solution.py:206
  419.4 13.4 %collective-permute-done.13.refs_7_.refs_15_ = bf16[96,6144]{1,0:T(8,128)(2,1)} collective-permute-done((bf16[96,6144]{1,0:T(8,128)(2,1)}, bf16[96,6144]{1,0:T(8,128)(2,1)}, u32[]{:S(2)}, u32[]{:S(2)}) %collective-permute-start.13) | collective-permute-done | bytes 1179680 | tf_op jit(solution)/shard_map/ppermute | solution.py:268
  432.8 7.5 %unpack.1 = (bf16[256,3072]{1,0:T(8,128)(2,1)}, bf16[256,3072]{1,0:T(8,128)(2,1)}) custom-call(s32[256,1]{1,0:T(8,128)} %copy.21.slot_ref, bf16[96,6144]{1,0:T(8,128)(2,1)} %get-tuple-element.48.refs_0_.refs_8_, bf16[96,6144]{1,0:T(8,128)(2,1)} %collective-permute-done.1.refs_1_.refs_9_, bf16[96,6144]{1,0:T(8,128)(2,1)} %copy-done.3, ...), custom_call_target="tpu_custom_call" | custom-call | flops 2415919104 | bytes 12582912 | tf_op jit(solution)/shard_map/unpack/pallas_call | solution.py:72
  (30 shorter events, 0.9 us)
Async XLA Ops:
  2.8 10.6 %copy-start.6 = (s32[256]{0:T(256)S(1)}, s32[256]{0:T(256)}, u32[]{:S(2)}) copy-start(s32[256]{0:T(256)} %multiply_add_fusion) | copy-start | bytes 3076
  9.9 4.3 collective-permute-start
  9.9 107.7 %collective-permute-start.2 = (bf16[96,6272]{1,0:T(8,128)(2,1)}, bf16[96,6272]{1,0:T(8,128)(2,1)S(1)}, u32[]{:S(2)}, u32[]{:S(2)}) collective-permute-start(bf16[96,6272]{1,0:T(8,128)(2,1)} %get-tuple-element.50), channel_id=1, source_target_pairs={{0,2},{1,3},{2,4},{3,5},{4,6},{5,7},{6,0},{7,1},{8,10},{9,11},{10,... | collective-permute-start | bytes 3612680 | tf_op jit(solution)/shard_map/ppermute | solution.py:265
  10.0 109.9 %collective-permute-start.3 = (bf16[96,6272]{1,0:T(8,128)(2,1)}, bf16[96,6272]{1,0:T(8,128)(2,1)}, u32[]{:S(2)}, u32[]{:S(2)}) collective-permute-start(bf16[96,6272]{1,0:T(8,128)(2,1)} %get-tuple-element.51), channel_id=1, source_target_pairs={{0,3},{1,2},{2,5},{3,4},{4,7},{5,6},{6,1},{7,0},{8,11},{9,10},{10,... | collective-permute-start | bytes 3612680 | tf_op jit(solution)/shard_map/ppermute | solution.py:265
  11.5 109.1 %collective-permute-start.4 = (bf16[96,6272]{1,0:T(8,128)(2,1)}, bf16[96,6272]{1,0:T(8,128)(2,1)}, u32[]{:S(2)}, u32[]{:S(2)}) collective-permute-start(bf16[96,6272]{1,0:T(8,128)(2,1)} %get-tuple-element.52), channel_id=1, source_target_pairs={{0,6},{1,7},{2,0},{3,1},{4,2},{5,3},{6,4},{7,5},{8,14},{9,15},{10,... | collective-permute-start | bytes 3612680 | tf_op jit(solution)/shard_map/ppermute | solution.py:265
  12.1 108.5 %collective-permute-start.5 = (bf16[96,6272]{1,0:T(8,128)(2,1)}, bf16[96,6272]{1,0:T(8,128)(2,1)}, u32[]{:S(2)}, u32[]{:S(2)}) collective-permute-start(bf16[96,6272]{1,0:T(8,128)(2,1)} %get-tuple-element.53), channel_id=1, source_target_pairs={{0,7},{1,6},{2,1},{3,0},{4,3},{5,2},{6,5},{7,4},{8,15},{9,14},{10,... | collective-permute-start | bytes 3612680 | tf_op jit(solution)/shard_map/ppermute | solution.py:265
  14.2 1.0 copy-start
  117.0 260.3 %collective-permute-start.1 = (bf16[96,6144]{1,0:T(8,128)(2,1)}, bf16[96,6144]{1,0:T(8,128)(2,1)}, u32[]{:S(2)}, u32[]{:S(2)}) collective-permute-start(bf16[96,6144]{1,0:T(8,128)(2,1)} %get-tuple-element.49), channel_id=1, source_target_pairs={{1,0},{0,1},{3,2},{2,3},{5,4},{4,5},{7,6},{6,7},{9,8},{8,9},{11,10... | collective-permute-start | bytes 3538952 | tf_op jit(solution)/shard_map/ppermute | solution.py:268
  117.6 3.0 copy-start.1
  117.6 155.6 %collective-permute-start.10 = (bf16[96,6272]{1,0:T(8,128)(2,1)}, bf16[96,6272]{1,0:T(8,128)(2,1)S(1)}, u32[]{:S(2)}, u32[]{:S(2)}) collective-permute-start(bf16[96,6272]{1,0:T(8,128)(2,1)} %get-tuple-element.61), channel_id=1, source_target_pairs={{0,4},{1,5},{2,6},{3,7},{4,0},{5,1},{6,2},{7,3},{8,12},{9,13},{10,... | collective-permute-start | bytes 3612680 | tf_op jit(solution)/shard_map/ppermute | solution.py:265
  119.9 154.8 %collective-permute-start.11 = (bf16[96,6272]{1,0:T(8,128)(2,1)}, bf16[96,6272]{1,0:T(8,128)(2,1)}, u32[]{:S(2)}, u32[]{:S(2)}) collective-permute-start(bf16[96,6272]{1,0:T(8,128)(2,1)} %get-tuple-element.62), channel_id=1, source_target_pairs={{0,5},{1,4},{2,7},{3,6},{4,1},{5,0},{6,3},{7,2},{8,13},{9,12},{10,... | collective-permute-start | bytes 3612680 | tf_op jit(solution)/shard_map/ppermute | solution.py:265
  270.8 107.8 %collective-permute-start.6 = (bf16[96,6144]{1,0:T(8,128)(2,1)}, bf16[96,6144]{1,0:T(8,128)(2,1)S(1)}, u32[]{:S(2)}, u32[]{:S(2)}) collective-permute-start(bf16[96,6144]{1,0:T(8,128)(2,1)} %get-tuple-element.54), channel_id=1, source_target_pairs={{2,0},{3,1},{4,2},{5,3},{6,4},{7,5},{0,6},{1,7},{10,8},{11,9},{12,... | collective-permute-start | bytes 3538952 | tf_op jit(solution)/shard_map/ppermute | solution.py:268
  271.5 147.8 %collective-permute-start.7 = (bf16[96,6144]{1,0:T(8,128)(2,1)}, bf16[96,6144]{1,0:T(8,128)(2,1)S(1)}, u32[]{:S(2)}, u32[]{:S(2)}) collective-permute-start(bf16[96,6144]{1,0:T(8,128)(2,1)} %get-tuple-element.55), channel_id=1, source_target_pairs={{3,0},{2,1},{5,2},{4,3},{7,4},{6,5},{1,6},{0,7},{11,8},{10,9},{13,... | collective-permute-start | bytes 3538952 | tf_op jit(solution)/shard_map/ppermute | solution.py:268
  273.2 2.4 copy-start.2
  273.2 146.2 %collective-permute-start.8 = (bf16[96,6144]{1,0:T(8,128)(2,1)}, bf16[96,6144]{1,0:T(8,128)(2,1)}, u32[]{:S(2)}, u32[]{:S(2)}) collective-permute-start(bf16[96,6144]{1,0:T(8,128)(2,1)} %get-tuple-element.56), channel_id=1, source_target_pairs={{6,0},{7,1},{0,2},{1,3},{2,4},{3,5},{4,6},{5,7},{14,8},{15,9},{8,1... | collective-permute-start | bytes 3538952 | tf_op jit(solution)/shard_map/ppermute | solution.py:268
  274.8 144.6 %collective-permute-start.9 = (bf16[96,6144]{1,0:T(8,128)(2,1)}, bf16[96,6144]{1,0:T(8,128)(2,1)}, u32[]{:S(2)}, u32[]{:S(2)}) collective-permute-start(bf16[96,6144]{1,0:T(8,128)(2,1)} %get-tuple-element.57), channel_id=1, source_target_pairs={{7,0},{6,1},{1,2},{0,3},{3,4},{2,5},{5,6},{4,7},{15,8},{14,9},{9,1... | collective-permute-start | bytes 3538952 | tf_op jit(solution)/shard_map/ppermute | solution.py:268
  377.3 42.0 %collective-permute-start.12 = (bf16[96,6144]{1,0:T(8,128)(2,1)}, bf16[96,6144]{1,0:T(8,128)(2,1)S(1)}, u32[]{:S(2)}, u32[]{:S(2)}) collective-permute-start(bf16[96,6144]{1,0:T(8,128)(2,1)} %get-tuple-element.63), channel_id=1, source_target_pairs={{4,0},{5,1},{6,2},{7,3},{0,4},{1,5},{2,6},{3,7},{12,8},{13,9},{14,... | collective-permute-start | bytes 3538952 | tf_op jit(solution)/shard_map/ppermute | solution.py:268
  378.5 13.1 %copy-start.3 = (bf16[96,6144]{1,0:T(8,128)(2,1)}, bf16[96,6144]{1,0:T(8,128)(2,1)S(1)}, u32[]{:S(2)}) copy-start(bf16[96,6144]{1,0:T(8,128)(2,1)S(1)} %collective-permute-done.6.refs_2_.refs_10_) | copy-start | bytes 3538948
  378.5 54.2 %collective-permute-start.13 = (bf16[96,6144]{1,0:T(8,128)(2,1)}, bf16[96,6144]{1,0:T(8,128)(2,1)}, u32[]{:S(2)}, u32[]{:S(2)}) collective-permute-start(bf16[96,6144]{1,0:T(8,128)(2,1)} %get-tuple-element.64), channel_id=1, source_target_pairs={{5,0},{4,1},{7,2},{6,3},{1,4},{0,5},{3,6},{2,7},{13,8},{12,9},{15,... | collective-permute-start | bytes 3538952 | tf_op jit(solution)/shard_map/ppermute | solution.py:268
  419.3 13.4 %copy-start.4 = (bf16[96,6144]{1,0:T(8,128)(2,1)}, bf16[96,6144]{1,0:T(8,128)(2,1)S(1)}, u32[]{:S(2)}) copy-start(bf16[96,6144]{1,0:T(8,128)(2,1)S(1)} %collective-permute-done.7.refs_3_.refs_11_) | copy-start | bytes 3538948
  419.4 13.4 %copy-start.5 = (bf16[96,6144]{1,0:T(8,128)(2,1)}, bf16[96,6144]{1,0:T(8,128)(2,1)S(1)}, u32[]{:S(2)}) copy-start(bf16[96,6144]{1,0:T(8,128)(2,1)S(1)} %collective-permute-done.12.refs_6_.refs_14_) | copy-start | bytes 3538948
